TPU v7x, 256 devices: a whole 4x4x8 slice. The times are simulated.
256 devices in a mesh: section: 16 (over z, x_lo), fsdp: 16 (over x_hi, y, core).
Axes of the slice: x: 4 (x_hi: 2, x_lo: 2; x = x_hi * 2 + x_lo), y: 4, z: 8, core: 2. Of those that a mesh axis runs over, the one named last changes fastest.
Arguments:
- layer_inputs: bfloat16 [16, 2, 6144, 2048], P('section', None, 'fsdp'), may hold values from -6 to 6
- out_grads: bfloat16 [16, 2, 6144, 2048], P('section', None, 'fsdp'), may hold values from -6 to 6
- attn_stash: bfloat16 [16, 2, 6144, 1024], P('section', None, 'fsdp'), may hold values from -6 to 6
- proj_grads: bfloat16 [16, 2, 6144, 1536], P('section', None, 'fsdp'), may hold values from -6 to 6
- w_qkv: bfloat16 [16, 2048, 1536], P('section', 'fsdp'), may hold values from -0.125 to 0.125
- w_out: bfloat16 [16, 1024, 2048], P('section', 'fsdp'), may hold values from -0.1875 to 0.1875
- norm_gain: float32 [16, 2048], P('section'), may hold values from 0.25 to 1.75
- b_sched: int32 [16], P('section'), may hold values from 0 to 1
- w_sched: int32 [16], P('section'), may hold values from 0 to 1
Outputs:
- prev_grads: bfloat16 [16, 6144, 2048], P('section', 'fsdp')
- grad_qkv: float32 [16, 2048, 1536], P('section', 'fsdp')
- grad_out: float32 [16, 1024, 2048], P('section', 'fsdp')
All inputs are finite; a program needn't handle non-finite values.
Results may differ from a plain program's by a relative error of at most 0.012.
Values may be sent and summed in bfloat16 or wider, within the bound.
No kernel may reach another device: no remote copies, remote signals or barrier semaphores. Data moves between devices by JAX's collectives and lax.ppermute only.
A program may use at most 128 MiB of HBM per device.

v0:
```python
import jax
import jax.numpy as jnp
from jax import lax
from jax.sharding import Mesh
from jax.sharding import PartitionSpec as P

HEAD_DIM = 64
HEADS = 16
KV_HEADS = 4
FSDP = ("fsdp_0", "fsdp_1", "fsdp_2")
rms_eps = 1e-05
rope_base = 500000.0


def passed_along(array, axis, by):
    size = lax.axis_size(axis)
    return lax.ppermute(array, axis, [(i, (i + by) % size) for i in range(size)])


def cut_along(array, dim, size):
    before, after = (array.shape[:dim], array.shape[dim + 1 :])
    return jnp.moveaxis(array.reshape(*before, size, -1, *after), dim, 0)


def summed_rows(array, chips, core, dim):
    sizes = (lax.axis_size(chips), lax.axis_size(core))
    parts = cut_along(array, dim, sizes[0] * sizes[1])
    inside = parts.shape[1:]
    parts = parts.reshape(*sizes, *inside).swapaxes(0, 1).reshape(-1, *inside)
    parts = lax.psum_scatter(parts, core, scatter_dimension=0, tiled=True)
    return lax.psum_scatter(parts, chips, scatter_dimension=0, tiled=True)[0]


def rope_tables(length, head_size):
    halfway = head_size // 2
    indices = jnp.arange(halfway, dtype=jnp.float32)
    frequency = rope_base ** (-2.0 * indices / head_size)
    angles = jnp.arange(length, dtype=jnp.float32)[:, None] * frequency[None, :]
    angles = jnp.concatenate([angles, angles], axis=1)
    return (jnp.cos(angles), jnp.sin(angles))


def rotate_half(values):
    halfway = values.shape[-1] // 2
    return jnp.concatenate([-values[..., halfway:], values[..., :halfway]], axis=-1)


def apply_rope(values, cosine_table, sine_table):
    return values * cosine_table[:, None, :] + rotate_half(values) * sine_table[:, None, :]


def unapply_rope(values, cosine_table, sine_table):
    return values * cosine_table[:, None, :] - rotate_half(values * sine_table[:, None, :])


def contract(pattern, first_operand, second_operand):
    return jnp.einsum(pattern, first_operand, second_operand, preferred_element_type=jnp.float32)


def normalize(inputs, gain_values):
    widened = inputs.astype(jnp.float32)
    inv_rms = lax.rsqrt(jnp.mean(widened * widened, axis=-1, keepdims=True) + rms_eps)
    normed = (widened * inv_rms * gain_values).astype(jnp.bfloat16)
    return (widened, inv_rms, normed)


def attention_back(qkv_rows, attn_grad, cosine_table, sine_table):
    tokens_here = qkv_rows.shape[0]
    q_width = HEADS * HEAD_DIM
    kv_width = KV_HEADS * HEAD_DIM
    group_size = HEADS // KV_HEADS
    score_scale = HEAD_DIM ** (-0.5)
    queries = apply_rope(
        qkv_rows[:, :q_width].reshape(tokens_here, HEADS, HEAD_DIM), cosine_table, sine_table
    ).astype(jnp.bfloat16)
    key_heads = apply_rope(
        qkv_rows[:, q_width : q_width + kv_width].reshape(tokens_here, KV_HEADS, HEAD_DIM),
        cosine_table,
        sine_table,
    ).astype(jnp.bfloat16)
    values = (
        qkv_rows[:, q_width + kv_width :]
        .reshape(tokens_here, KV_HEADS, HEAD_DIM)
        .astype(jnp.bfloat16)
    )
    queries = queries.reshape(tokens_here, KV_HEADS, group_size, HEAD_DIM)
    grad_heads = attn_grad.reshape(tokens_here, KV_HEADS, group_size, HEAD_DIM)
    scores = contract("tkgd,ukd->kgtu", queries, key_heads) * score_scale
    row_ids = lax.broadcasted_iota(jnp.int32, (tokens_here, tokens_here), 0)
    col_ids = lax.broadcasted_iota(jnp.int32, (tokens_here, tokens_here), 1)
    causal = col_ids <= row_ids
    exp_scores = jnp.where(causal, jnp.exp(scores), 0.0)
    attention = exp_scores / jnp.sum(exp_scores, axis=-1, keepdims=True)
    attention_low = attention.astype(jnp.bfloat16)
    grad_values = contract("kgtu,tkgd->ukd", attention_low, grad_heads)
    grad_attention = contract("tkgd,ukd->kgtu", grad_heads, values)
    row_delta = jnp.sum(attention * grad_attention, axis=-1, keepdims=True)
    grad_scores = (attention * (grad_attention - row_delta) * score_scale).astype(jnp.bfloat16)
    grad_queries = contract("kgtu,ukd->tkgd", grad_scores, key_heads)
    grad_keys = contract("kgtu,tkgd->ukd", grad_scores, queries)
    grad_queries = unapply_rope(
        grad_queries.reshape(tokens_here, HEADS, HEAD_DIM), cosine_table, sine_table
    )
    grad_keys = unapply_rope(grad_keys, cosine_table, sine_table)
    joined = jnp.concatenate(
        [
            grad_queries.reshape(tokens_here, q_width),
            grad_keys.reshape(tokens_here, kv_width),
            grad_values.reshape(tokens_here, kv_width),
        ],
        axis=1,
    )
    return joined.astype(jnp.bfloat16)


def finish_grad(widened, inv_rms, gain_values, upstream, grad_normed):
    scaled = grad_normed * gain_values
    inner_mean = jnp.mean(scaled * widened, axis=-1, keepdims=True)
    result = upstream.astype(jnp.float32) + inv_rms * scaled - widened * inv_rms**3 * inner_mean
    return result.astype(jnp.bfloat16)


def local(
    layer_inputs, out_grads, attn_stash, proj_grads, w_qkv, w_out, norm_gain, b_sched, w_sched
):
    seq_len = layer_inputs.shape[2]
    cosine_table, sine_table = rope_tables(seq_len, HEAD_DIM)
    gain_values = norm_gain[0]
    b_slot = b_sched[0]
    w_slot = w_sched[0]
    qkv_shard = w_qkv[0]
    out_shard = w_out[0]
    contract_rows = (((0,), (0,)), ((), ()))
    contract_cols = (((1,), (1,)), ((), ()))
    inputs_b = lax.dynamic_index_in_dim(layer_inputs[0], b_slot, 0, keepdims=False)
    upstream_b = lax.dynamic_index_in_dim(out_grads[0], b_slot, 0, keepdims=False)
    widened, inv_rms, normed = normalize(inputs_b, gain_values)
    whole_qkv = lax.all_gather(qkv_shard, FSDP, axis=0, tiled=True)
    qkv_rows = jnp.dot(normed, whole_qkv, preferred_element_type=jnp.float32)
    attn_grad = lax.dot_general(
        upstream_b,
        lax.all_gather(out_shard, FSDP, axis=0, tiled=True),
        contract_cols,
        preferred_element_type=jnp.float32,
    ).astype(jnp.bfloat16)
    grad_proj = attention_back(qkv_rows, attn_grad, cosine_table, sine_table)
    grad_normed = lax.dot_general(
        grad_proj, whole_qkv, contract_cols, preferred_element_type=jnp.float32
    )
    sent_grads = finish_grad(widened, inv_rms, gain_values, upstream_b, grad_normed)
    sent_back = passed_along(sent_grads, "section", -1)[None]
    inputs_w = lax.dynamic_index_in_dim(layer_inputs[0], w_slot, 0, keepdims=False)
    upstream_w = lax.dynamic_index_in_dim(out_grads[0], w_slot, 0, keepdims=False)
    attended_w = lax.dynamic_index_in_dim(attn_stash[0], w_slot, 0, keepdims=False)
    projected_w = lax.dynamic_index_in_dim(proj_grads[0], w_slot, 0, keepdims=False)
    unused_wide, unused_inv, normed_w = normalize(inputs_w, gain_values)
    rows_part = normed_w
    grad_qkv_w = lax.psum_scatter(
        lax.dot_general(
            rows_part, projected_w, contract_rows, preferred_element_type=jnp.float32
        ).astype(jnp.bfloat16),
        FSDP,
        scatter_dimension=0,
        tiled=True,
    ).astype(jnp.float32)
    rows_part = attended_w
    grad_out_w = summed_rows(
        lax.dot_general(
            rows_part, upstream_w, contract_rows, preferred_element_type=jnp.float32
        ).astype(jnp.bfloat16),
        ("fsdp_0", "fsdp_1"),
        "fsdp_2",
        0,
    ).astype(jnp.float32)
    grad_qkv_w, grad_out_w = (grad_qkv_w[None], grad_out_w[None])
    return (sent_back, grad_qkv_w, grad_out_w)


def solution(mesh):
    finer = Mesh(
        mesh.devices.reshape(mesh.shape["section"], 2, 4, 2),
        ("section", "fsdp_0", "fsdp_1", "fsdp_2"),
    )
    return jax.shard_map(
        local,
        mesh=finer,
        in_specs=(
            P("section", None, FSDP, None),
            P("section", None, FSDP, None),
            P("section", None, FSDP, None),
            P("section", None, FSDP, None),
            P("section", FSDP, None),
            P("section", FSDP, None),
            P("section", None),
            P("section"),
            P("section"),
        ),
        out_specs=(P("section", FSDP, None), P("section", FSDP, None), P("section", FSDP, None)),
        check_vma=False,
    )
```

profile of v0, /device:TPU:1, one launch (start us, length us, event | category | flops | bytes accessed | tf_op | source)
XLA Modules:
  0.0 281.7 jit_solution(17291368382302800708)
XLA Ops:
  8.0 0.0 all-gather.7.cloned.1.call-start
  8.1 0.7 all-gather.7.cloned.1.call-update
  8.7 0.0 reduce-scatter.6.cloned.1.call-start
  9.4 4.0 %convolution_convert_fusion.1 = bf16[1024,2048]{1,0:T(8,128)(2,1)S(1)} fusion(bf16[1,2,384,2048]{3,2,1,0:T(8,128)(2,1)} %param.10, s32[]{:T(128)S(6)} %select_n.19, bf16[1,2,384,1024]{3,2,1,0:T(8,128)(2,1)} %param.11), kind=kOutput, calls=%fused_computation.27 | convolution fusion | flops 1612709888 | bytes 6554624 | tf_op jit(solution)/shard_map/dot_general | solution.py:168
  13.5 2.3 copy.33
  15.8 0.0 all-gather.5.cloned.1.call-start
  15.9 0.7 all-gather.5.cloned.1.call-update
  16.6 0.0 reduce-scatter.4.cloned.1.call-start
  16.6 1.8 fusion.17
  18.4 7.2 %convolution_convert_fusion = bf16[2048,1536]{1,0:T(8,128)(2,1)} fusion(f32[2048]{0:T(1024)S(1)} %bitcast.182, f32[384]{0:T(512)S(1)} %add_rsqrt_fusion, bf16[1,2,384,2048]{3,2,1,0:T(8,128)(2,1)} %param.9, s32[]{:T(128)S(6)} %select_n.19, bf16[1,2,384,1536]{3,2,1,0:T(8,128)(2,1)S(1)} %copy-done), kind=kOutput, calls=%fused_computation.9 | convolution fusion | flops 2422210560 | bytes 9055232 | tf_op jit(solution)/shard_map/dot_general | solution.py:159
  25.7 0.0 reduce-scatter.8.cloned.1.call-start
  26.4 1.8 fusion.20
  28.2 0.7 iota_compare_fusion
  28.9 0.1 iota_multiply_fusion
  29.0 0.9 fusion.74
  29.9 45.8 %all-gather.7.cloned.1.call-done = bf16[1,1024,2048]{2,1,0:T(8,128)(2,1)} async-done(((bf16[1,64,2048]{2,1,0:T(8,128)(2,1)}), bf16[1,1024,2048]{2,1,0:T(8,128)(2,1)}) %all-gather.7.cloned.1.call-update) | async-done | bytes 4194320 | tf_op jit(solution)/shard_map/all_gather | solution.py:142
  75.7 4.5 %fusion.45 = bf16[384,1024]{1,0:T(8,128)(2,1)S(1)} fusion(bf16[1,1024,2048]{2,1,0:T(8,128)(2,1)} %all-gather.7.cloned.1.call-done, bf16[1,2,384,2048]{3,2,1,0:T(8,128)(2,1)} %param.10, s32[]{:T(128)S(6)} %select_n.17), kind=kOutput, calls=%fused_computation.56 | convolution fusion | flops 1611005952 | bytes 6553604 | tf_op jit(solution)/shard_map/dot_general | solution.py:140
  80.1 0.4 copy.29
  80.6 79.5 %all-gather.5.cloned.1.call-done = bf16[1,2048,1536]{2,1,0:T(8,128)(2,1)} async-done(((bf16[1,128,1536]{2,1,0:T(8,128)(2,1)}), bf16[1,2048,1536]{2,1,0:T(8,128)(2,1)}) %all-gather.5.cloned.1.call-update) | async-done | bytes 6291472 | tf_op jit(solution)/shard_map/all_gather | solution.py:138
  160.1 5.3 %fusion.8 = f32[384,1536]{1,0:T(8,128)S(1)} fusion(bf16[1,2048,1536]{2,1,0:T(8,128)(2,1)} %all-gather.5.cloned.1.call-done, f32[2048]{0:T(1024)S(1)} %bitcast.183, f32[384]{0:T(512)S(1)} %get-tuple-element.14, bf16[1,2,384,2048]{3,2,1,0:T(8,128)(2,1)} %param.9, s32[]{:T(128)S(6)} %select_n.17), kind=kOutput, calls=%fused_computation.12 | convolution fusion | flops 2419064832 | bytes 10233348 | tf_op jit(solution)/shard_map/dot_general | solution.py:139
  165.4 1.3 slice.48
  166.7 0.7 slice.61
  167.4 0.2 copy.25
  167.5 0.8 slice_negate_fusion.3
  168.3 1.9 copy.26
  170.2 1.0 slice_negate_fusion.1
  171.2 1.7 copy.28
  173.0 6.1 %fusion.89 = f32[4,384,384,4]{2,1,3,0:T(8,128)} fusion(bf16[384,4,64,1]{0,2,3,1:T(8,128)(2,1)} %bitcast.178, bf16[384,4,4,64]{0,3,2,1:T(8,128)(2,1)S(1)} %bitcast.171), kind=kOutput, calls=%fused_computation.104 | convolution fusion | flops 301989888 | bytes 10420224 | tf_op jit(solution)/shard_map/tkgd,ukd->kgtu/dot_general | solution.py:57
  179.1 0.1 fusion.72
  179.2 0.3 fusion.34
  179.5 0.5 copy-done.15
  180.0 5.8 %fusion.5 = (f32[4,4,384]{2,1,0:T(4,128)S(1)}, f32[4,384,384,4]{2,1,3,0:T(8,128)}) fusion(pred[384,384]{0,1:T(8,128)(4,1)S(1)} %copy-done.15, bf16[384,4,64,1]{0,2,3,1:T(8,128)(2,1)S(1)} %fusion.72, bf16[384,4,4,64]{0,3,2,1:T(8,128)(2,1)S(1)} %fusion.34), kind=kOutput, calls=%fused_computation.8 | convolution fusion | flops 309061632 | bytes 10592256 | tf_op jit(solution)/shard_map/tkgd,ukd->kgtu/dot_general | solution.py:57
  185.8 18.0 %broadcast_multiply_fusion = (f32[384,4,64]{0,2,1:T(8,128)S(1)}, f32[384,4,64]{0,2,1:T(8,128)S(1)}) fusion(f32[384,64]{0,1:T(8,128)S(1)} %copy-done.8, bf16[384,4,4,64]{0,3,2,1:T(8,128)(2,1)} %copy-done.12, f32[4,384,384,4]{2,1,3,0:T(8,128)} %fusion.89, f32[4,4,384]{2,1,0:T(4,128)S(1)} %get-tuple-element.15, f32[4,384,384,4]{2,1,3,0:T(8,128)} %get-tuple-element.16, ...), kind=kOutput, calls=%fused_computation.85 | convolution fusion | flops 328046976 | bytes 20717568 | tf_op jit(solution)/shard_map/kgtu,tkgd->ukd/dot_general | solution.py:57
  203.8 16.2 %fusion.16 = f32[4,64,4,384]{3,1,2,0:T(8,128)} fusion(bf16[384,4,64,1]{0,2,3,1:T(8,128)(2,1)S(1)} %copy-done.14, f32[4,384,384,4]{2,1,3,0:T(8,128)} %fusion.89, f32[4,384,384,4]{2,1,3,0:T(8,128)} %get-tuple-element.16, f32[4,4,384]{2,1,0:T(4,128)S(1)} %get-tuple-element.15, pred[384,384]{0,1:T(8,128)(4,1)S(1)} %copy-done.16), kind=kOutput, calls=%fused_computation.24 | convolution fusion | flops 327948672 | bytes 20815872 | tf_op jit(solution)/shard_map/kgtu,ukd->tkgd/dot_general | solution.py:57
  220.1 1.5 bitcast_multiply_fusion.8
  221.6 0.1 slice_negate_fusion
  221.8 0.1 pad_maximum_fusion
  221.9 1.2 copy-done.3
  223.0 0.3 fusion.36
  223.3 0.1 fusion.71
  223.4 6.2 %fusion.63 = bf16[4,64,384]{2,1,0:T(8,128)(2,1)S(1)} fusion(bf16[384,4,4,64]{0,3,2,1:T(8,128)(2,1)S(1)} %bitcast.172, f32[4,384,384,4]{2,1,3,0:T(8,128)} %get-tuple-element.16, f32[4,4,384]{2,1,0:T(4,128)S(1)} %get-tuple-element.15, pred[384,384]{0,1:T(8,128)(4,1)S(1)} %copy-done.16), kind=kOutput, calls=%fused_computation.68 | convolution fusion | flops 311525376 | bytes 10592256 | tf_op jit(solution)/shard_map/kgtu,tkgd->ukd/dot_general | solution.py:57
  229.7 2.8 fusion.26
  232.5 2.0 fusion.25
  234.6 3.0 %collective-permute-start = (bf16[384,2048]{1,0:T(8,128)(2,1)}, bf16[384,2048]{1,0:T(8,128)(2,1)}, u32[]{:S(2)}, u32[]{:S(2)}) collective-permute-start(bf16[384,2048]{1,0:T(8,128)(2,1)} %fusion.25), channel_id=1, source_target_pairs={{0,240},{16,0},{32,16},{48,32},{64,48},{80,64},{96,80},{112,96},{1... | collective-permute-start | bytes 4718600 | tf_op jit(solution)/shard_map/ppermute | solution.py:17
  237.6 2.0 bitcast_convert_fusion
  239.6 1.8 convert_element_type.74
  241.3 30.0 %collective-permute-done = bf16[384,2048]{1,0:T(8,128)(2,1)} collective-permute-done((bf16[384,2048]{1,0:T(8,128)(2,1)}, bf16[384,2048]{1,0:T(8,128)(2,1)}, u32[]{:S(2)}, u32[]{:S(2)}) %collective-permute-start) | collective-permute-done | bytes 1572896 | tf_op jit(solution)/shard_map/ppermute | solution.py:17
  271.4 2.7 copy.44
  (51 shorter events, 0.3 us)
Async XLA Ops:
  8.0 10.4 %copy-start = (bf16[1,2,384,1536]{3,2,1,0:T(8,128)(2,1)S(1)}, bf16[1,2,384,1536]{3,2,1,0:T(8,128)(2,1)}, u32[]{:S(2)}) copy-start(bf16[1,2,384,1536]{3,2,1,0:T(8,128)(2,1)} %param.12) | copy-start | bytes 7077892
  8.0 67.6 %all-gather.7.cloned.1.call-start = ((), (), s32[]{:S(2)}) async-start(), calls=%async_computation.7 | async-start | bytes 4456448 | tf_op jit(solution)/shard_map/all_gather | solution.py:142
  8.7 71.8 %reduce-scatter.6.cloned.1.call-start = ((), (), s32[]{:S(2)}) async-start(), calls=%async_computation.4 | async-start | bytes 6291456 | tf_op jit(solution)/shard_map/reduce_scatter | solution.py:30
  15.8 2.6 copy-start.17
  15.8 144.3 %all-gather.5.cloned.1.call-start = ((), (), s32[]{:S(2)}) async-start(), calls=%async_computation.6 | async-start | bytes 6684672 | tf_op jit(solution)/shard_map/all_gather | solution.py:138
  16.6 221.0 %reduce-scatter.4.cloned.1.call-start = ((), (), s32[]{:S(2)}) async-start(), calls=%async_computation.3 | async-start | bytes 6684672 | tf_op jit(solution)/shard_map/reduce_scatter | solution.py:158
  25.7 213.9 %reduce-scatter.8.cloned.1.call-start = ((), (), s32[]{:S(2)}) async-start(), calls=%async_computation.5 | async-start | bytes 2359296 | tf_op jit(solution)/shard_map/reduce_scatter | solution.py:31
  173.0 6.2 %copy-start.5 = (f32[384,64]{0,1:T(8,128)S(1)}, f32[384,64]{0,1:T(8,128)}, u32[]{:S(2)}) copy-start(f32[384,64]{0,1:T(8,128)} %get-tuple-element.11) | copy-start | bytes 294916
  173.0 6.2 %copy-start.7 = (f32[384,64]{0,1:T(8,128)S(1)}, f32[384,64]{0,1:T(8,128)}, u32[]{:S(2)}) copy-start(f32[384,64]{0,1:T(8,128)} %get-tuple-element.12) | copy-start | bytes 294916
  173.0 6.2 %copy-start.9 = (f32[384,4,32]{0,2,1:T(8,128)S(1)}, f32[384,4,32]{0,2,1:T(8,128)}, u32[]{:S(2)}) copy-start(f32[384,4,32]{0,2,1:T(8,128)} %get-tuple-element.9) | copy-start | bytes 589828
  173.0 6.2 %copy-start.10 = (f32[384,4,32]{0,2,1:T(8,128)S(1)}, f32[384,4,32]{0,2,1:T(8,128)}, u32[]{:S(2)}) copy-start(f32[384,4,32]{0,2,1:T(8,128)} %get-tuple-element.10) | copy-start | bytes 589828
  173.0 6.2 %copy-start.4 = (f32[384,16,32]{0,2,1:T(8,128)S(1)}, f32[384,16,32]{0,2,1:T(8,128)}, u32[]{:S(2)}) copy-start(f32[384,16,32]{0,2,1:T(8,128)} %get-tuple-element.6) | copy-start | bytes 2359300
  179.1 0.9 copy-start.15
  179.2 6.6 %copy-start.13 = (bf16[384,4,64,1]{0,2,3,1:T(8,128)(2,1)}, bf16[384,4,64,1]{0,2,3,1:T(8,128)(2,1)S(1)}, u32[]{:S(2)}) copy-start(bf16[384,4,64,1]{0,2,3,1:T(8,128)(2,1)S(1)} %fusion.72) | copy-start | bytes 589828
  180.0 5.8 %copy-start.12 = (bf16[384,4,4,64]{0,3,2,1:T(8,128)(2,1)}, bf16[384,4,4,64]{0,3,2,1:T(8,128)(2,1)S(1)}, u32[]{:S(2)}) copy-start(bf16[384,4,4,64]{0,3,2,1:T(8,128)(2,1)S(1)} %fusion.34) | copy-start | bytes 2359300
  180.0 5.8 %copy-start.8 = (f32[384,64]{0,1:T(8,128)S(1)}, f32[384,64]{0,1:T(8,128)}, u32[]{:S(2)}) copy-start(f32[384,64]{0,1:T(8,128)} %get-tuple-element.12) | copy-start | bytes 294916
  180.0 5.8 %copy-start.16 = (pred[384,384]{0,1:T(8,128)(4,1)S(1)}, pred[384,384]{0,1:T(8,128)(4,1)}, u32[]{:S(2)}) copy-start(pred[384,384]{0,1:T(8,128)(4,1)} %iota_compare_fusion) | copy-start | bytes 442372
  185.8 18.0 %copy-start.14 = (bf16[384,4,64,1]{0,2,3,1:T(8,128)(2,1)S(1)}, bf16[384,4,64,1]{0,2,3,1:T(8,128)(2,1)}, u32[]{:S(2)}) copy-start(bf16[384,4,64,1]{0,2,3,1:T(8,128)(2,1)} %copy-done.13) | copy-start | bytes 589828
  221.6 1.4 copy-start.3
  221.6 1.4 copy-start.6
  223.0 6.6 %slice-start = ((s8[6291456]{0:T(1024)(128)(4,1)}), s8[4194304]{0:T(1024)(128)(4,1)S(1)}, s32[]{:S(2)}) async-start(s8[6291456]{0:T(1024)(128)(4,1)} %bitcast.180), calls=%async_computation.8 | async-start | bytes 8388608
  223.4 6.3 %copy-start.2 = (bf16[1,2,384,2048]{3,2,1,0:T(8,128)(2,1)S(1)}, bf16[1,2,384,2048]{3,2,1,0:T(8,128)(2,1)}, u32[]{:S(2)}) copy-start(bf16[1,2,384,2048]{3,2,1,0:T(8,128)(2,1)} %param.9) | copy-start | bytes 9437188
  223.4 6.3 %slice-start.1 = ((s8[6291456]{0:T(1024)(128)(4,1)}), s8[2097152]{0:T(1024)(128)(4,1)S(1)}, s32[]{:S(2)}) async-start(s8[6291456]{0:T(1024)(128)(4,1)} %bitcast.180), calls=%async_computation.9 | async-start | bytes 4194304
  229.7 2.8 %copy-start.11 = (bf16[1,2,384,2048]{3,2,1,0:T(8,128)(2,1)S(1)}, bf16[1,2,384,2048]{3,2,1,0:T(8,128)(2,1)}, u32[]{:S(2)}) copy-start(bf16[1,2,384,2048]{3,2,1,0:T(8,128)(2,1)} %param.10) | copy-start | bytes 9437188
  232.5 41.6 %copy-start.1 = (bf16[1,2,384,1536]{3,2,1,0:T(8,128)(2,1)S(1)}, bf16[1,2,384,1536]{3,2,1,0:T(8,128)(2,1)}, u32[]{:S(2)}) copy-start(bf16[1,2,384,1536]{3,2,1,0:T(8,128)(2,1)} %param.12) | copy-start | bytes 7077892
  234.6 36.8 %collective-permute-start = (bf16[384,2048]{1,0:T(8,128)(2,1)}, bf16[384,2048]{1,0:T(8,128)(2,1)}, u32[]{:S(2)}, u32[]{:S(2)}) collective-permute-start(bf16[384,2048]{1,0:T(8,128)(2,1)} %fusion.25), channel_id=1, source_target_pairs={{0,240},{16,0},{32,16},{48,32},{64,48},{80,64},{96,80},{112,96},{1... | collective-permute-start | bytes 4718600 | tf_op jit(solution)/shard_map/ppermute | solution.py:17
Sparse Core Ops, SparseCore 0:
  11.6 64.0 all-gather.6
  78.4 81.6 all-gather.4
Sparse Core Ops, SparseCore 1:
  15.9 21.8 reduce-scatter.5
  42.1 99.7 reduce-scatter.3
  145.7 81.1 reduce-scatter.7
where the time goes:
time: 282 us
  waiting for transfers between devices  157 us (56%)
  matrix products  76.1 us (27%)
  between operations  17.3 us (6%)
  other arithmetic  15.3 us (5%)
  local copies, waits for them, and re-layouts  12.9 us (5%)
  starting transfers between devices  3.24 us (1%)
    all_gather x1, waiting for transfers between devices, local(): whole_qkv = lax.all_gather(qkv_shard, FSDP, axis=0, tiled=True)  79.5 us
    dot_general x5, matrix products, contract(): jnp.einsum(pattern, first_operand, second_operand, preferred_element_type...  52.3 us
    all_gather x1, waiting for transfers between devices, local(): lax.all_gather(out_shard, FSDP, axis=0, tiled=True)  45.8 us
    ppermute x1, waiting for transfers between devices, passed_along(): lax.ppermute(array, axis, [(i, (i + by) % size) for i in range(size)])  30 us
    dot_general x1, matrix products, local(): lax.dot_general(rows_part, projected_w, contract_rows, preferred_element_...  7.19 us
  transfers between devices with their start and end apart: 6, of which 3 were waited for; matrix products, arithmetic and copies ran while one was open for 35% of the time, Pallas kernels for 0%

commit v1 on v0

--- a/solution.py
+++ b/solution.py
@@ -135,7 +135,8 @@
     inputs_b = lax.dynamic_index_in_dim(layer_inputs[0], b_slot, 0, keepdims=False)
     upstream_b = lax.dynamic_index_in_dim(out_grads[0], b_slot, 0, keepdims=False)
     widened, inv_rms, normed = normalize(inputs_b, gain_values)
-    whole_qkv = lax.all_gather(qkv_shard, FSDP, axis=0, tiled=True)
+    outgoing = jnp.stack([qkv_shard] * lax.axis_size(FSDP))
+    whole_qkv = jnp.concatenate(lax.all_to_all(outgoing, FSDP, 0, 0), axis=0)
     qkv_rows = jnp.dot(normed, whole_qkv, preferred_element_type=jnp.float32)
     attn_grad = lax.dot_general(
         upstream_b,

time: 282 us -> 323 us (1.15)
  waiting for transfers between devices: 157 us -> 193 us
  starting transfers between devices: 3.24 us -> 9.91 us
  other arithmetic: 15.3 us -> 12 us
    all_to_all x0 -> x1, waiting for transfers between devices: none -> 99 us  [local(): whole_qkv = jnp.concatenate(lax.all_to_all(outgoing, FSDP, 0, 0), axis=0)]
    all_gather x1 -> x0, waiting for transfers between devices: 79.5 us -> none  [local(): whole_qkv = lax.all_gather(qkv_shard, FSDP, axis=0, tiled=True)]
    reduce_scatter x1, waiting for transfers between devices: 0.01 us -> 50.2 us  [summed_rows(): return lax.psum_scatter(parts, chips, scatter_dimension=0, tiled=True)[0]]
    all_gather x1, waiting for transfers between devices: 45.8 us -> 0.01 us  [local(): lax.all_gather(out_shard, FSDP, axis=0, tiled=True)]
    ppermute x1, waiting for transfers between devices: 30 us -> 43 us  [passed_along(): lax.ppermute(array, axis, [(i, (i + by) % size) for i in range(size)])]
    all_to_all x0 -> x1, starting transfers between devices: none -> 8.57 us  [local(): whole_qkv = jnp.concatenate(lax.all_to_all(outgoing, FSDP, 0, 0), axis=0)]
    dot_general x5, matrix products: 52.3 us -> 47.3 us  [contract(): jnp.einsum(pattern, first_operand, second_operand, preferred_element_type...]
    dot_general x1, matrix products: 2.81 us -> 6.26 us  [local(): lax.dot_general(grad_proj, whole_qkv, contract_cols, preferred_element_ty...]
  transfers between devices with their start and end apart: 6 -> 6, of which waited for: 3 -> 3; matrix products, arithmetic and copies ran while one was open for 35% -> 29% of each run, Pallas kernels for 0% -> 0%
where the time goes in v1:
time: 323 us
  waiting for transfers between devices  193 us (60%)
  matrix products  75.1 us (23%)
  between operations  17.2 us (5%)
  local copies, waits for them, and re-layouts  15.3 us (5%)
  other arithmetic  12 us (4%)
  starting transfers between devices  9.91 us (3%)
    all_to_all x1, waiting for transfers between devices, local(): whole_qkv = jnp.concatenate(lax.all_to_all(outgoing, FSDP, 0, 0), axis=0)  99 us
    reduce_scatter x1, waiting for transfers between devices, summed_rows(): return lax.psum_scatter(parts, chips, scatter_dimension=0, tiled=True)[0]  50.2 us
    dot_general x5, matrix products, contract(): jnp.einsum(pattern, first_operand, second_operand, preferred_element_type...  47.3 us
    ppermute x1, waiting for transfers between devices, passed_along(): lax.ppermute(array, axis, [(i, (i + by) % size) for i in range(size)])  43 us
    all_to_all x1, starting transfers between devices, local(): whole_qkv = jnp.concatenate(lax.all_to_all(outgoing, FSDP, 0, 0), axis=0)  8.57 us
    dot_general x1, matrix products, local(): lax.dot_general(rows_part, projected_w, contract_rows, preferred_element_...  7.62 us
  transfers between devices with their start and end apart: 6, of which 3 were waited for; matrix products, arithmetic and copies ran while one was open for 29% of the time, Pallas kernels for 0%

profile of v1, /device:TPU:1, one launch (start us, length us, event | category | flops | bytes accessed | tf_op | source)
XLA Modules:
  0.0 322.5 jit_solution(12353337983986174524)
XLA Ops:
  8.0 0.0 all-gather.3.cloned.1.call-start
  8.1 0.7 all-gather.3.cloned.1.call-update
  8.7 0.0 reduce-scatter.6.cloned.1.call-start
  9.4 4.0 %convolution_convert_fusion.1 = bf16[1024,2048]{1,0:T(8,128)(2,1)S(1)} fusion(bf16[1,2,384,2048]{3,2,1,0:T(8,128)(2,1)} %param.10, s32[]{:T(128)S(6)} %select_n.19, bf16[1,2,384,1024]{3,2,1,0:T(8,128)(2,1)} %param.11), kind=kOutput, calls=%fused_computation.24 | convolution fusion | flops 1612709888 | bytes 6554624 | tf_op jit(solution)/shard_map/dot_general | solution.py:169
  13.5 2.3 copy.33
  15.8 1.0 copy-done.8
  16.8 3.3 %stack.3 = bf16[16,128,1536]{2,1,0:T(8,128)(2,1)} broadcast(bf16[128,1536]{1,0:T(8,128)(2,1)S(1)} %bitcast.186), dimensions={1,2} | broadcast | bytes 6684672 | tf_op jit(solution)/shard_map/stack | solution.py:138
  20.0 8.6 %all-to-all-start = ((bf16[16,128,1536]{2,1,0:T(8,128)(2,1)}), bf16[16,128,1536]{2,1,0:T(8,128)(2,1)}, u32[]{:S(2)}, u32[]{:S(2)}) async-start(bf16[16,128,1536]{2,1,0:T(8,128)(2,1)} %stack.3), calls=%async_computation | async-start | bytes 12582912 | tf_op jit(solution)/shard_map/all_to_all | solution.py:139
  28.6 0.0 reduce-scatter.4.cloned.1.call-start
  28.7 1.8 fusion.16
  30.5 7.6 %convolution_convert_fusion = bf16[2048,1536]{1,0:T(8,128)(2,1)} fusion(f32[384]{0:T(512)S(1)} %add_rsqrt_fusion, f32[2048]{0:T(1024)S(1)} %bitcast.188, bf16[1,2,384,2048]{3,2,1,0:T(8,128)(2,1)} %param.9, s32[]{:T(128)S(6)} %select_n.19, bf16[1,2,384,1536]{3,2,1,0:T(8,128)(2,1)S(1)} %copy-done), kind=kOutput, calls=%fused_computation.9 | convolution fusion | flops 2422210560 | bytes 9055232 | tf_op jit(solution)/shard_map/dot_general | solution.py:160
  38.2 0.2 reduce-scatter.8.cloned.1.call-start
  39.0 1.8 fusion.19
  40.9 0.1 iota_multiply_fusion
  41.0 0.2 fusion.71
  41.2 99.0 %all-to-all-done = bf16[16,128,1536]{2,1,0:T(8,128)(2,1)} async-done(((bf16[16,128,1536]{2,1,0:T(8,128)(2,1)}), bf16[16,128,1536]{2,1,0:T(8,128)(2,1)}, u32[]{:S(2)}, u32[]{:S(2)}) %all-to-all-start) | async-done | bytes 6291488 | tf_op jit(solution)/shard_map/all_to_all | solution.py:139
  140.2 5.4 %fusion.27 = f32[384,1536]{1,0:T(8,128)S(1)} fusion(bf16[2048,1536]{1,0:T(8,128)(2,1)} %bitcast.6, f32[2048]{0:T(1024)S(1)} %bitcast.189, f32[384]{0:T(512)S(1)} %get-tuple-element.14, bf16[1,2,384,2048]{3,2,1,0:T(8,128)(2,1)} %param.9, s32[]{:T(128)S(6)} %select_n.17), kind=kOutput, calls=%fused_computation.37 | convolution fusion | flops 2419064832 | bytes 10233348 | tf_op jit(solution)/shard_map/dot_general | solution.py:140
  145.6 1.3 slice.48
  146.9 0.2 copy.25
  147.1 1.9 copy.26
  149.0 0.2 copy.28
  149.3 0.1 fusion.69
  149.3 0.1 slice_negate_fusion.1
  149.4 0.3 fusion.32
  149.7 0.9 copy-done.5
  150.6 5.8 %fusion.5 = (f32[4,4,384]{2,1,0:T(4,128)S(1)}, f32[4,384,384,4]{2,1,3,0:T(8,128)}) fusion(pred[384,384]{0,1:T(8,128)(4,1)S(1)} %iota_compare_fusion, bf16[384,4,64,1]{0,2,3,1:T(8,128)(2,1)S(1)} %fusion.69, bf16[384,4,4,64]{0,3,2,1:T(8,128)(2,1)S(1)} %fusion.32), kind=kOutput, calls=%fused_computation.8 | convolution fusion | flops 309061632 | bytes 10592256 | tf_op jit(solution)/shard_map/tkgd,ukd->kgtu/dot_general | solution.py:57
  156.4 4.5 %fusion.42 = bf16[384,1024]{1,0:T(8,128)(2,1)S(1)} fusion(bf16[1,1024,2048]{2,1,0:T(8,128)(2,1)} %all-gather.3.cloned.1.call-done, bf16[1,2,384,2048]{3,2,1,0:T(8,128)(2,1)} %param.10, s32[]{:T(128)S(6)} %select_n.17), kind=kOutput, calls=%fused_computation.54 | convolution fusion | flops 1611005952 | bytes 6553604 | tf_op jit(solution)/shard_map/dot_general | solution.py:141
  160.9 0.4 copy.29
  161.3 5.1 %fusion.86 = f32[4,384,384,4]{2,1,3,0:T(8,128)} fusion(bf16[384,4,64,1]{0,2,3,1:T(8,128)(2,1)S(1)} %bitcast.185, bf16[384,4,4,64]{0,3,2,1:T(8,128)(2,1)S(1)} %bitcast.178), kind=kOutput, calls=%fused_computation.102 | convolution fusion | flops 301989888 | bytes 10420224 | tf_op jit(solution)/shard_map/tkgd,ukd->kgtu/dot_general | solution.py:57
  166.3 16.2 %fusion.12 = f32[4,64,4,384]{3,1,2,0:T(8,128)} fusion(bf16[384,4,64,1]{0,2,3,1:T(8,128)(2,1)S(1)} %fusion.69, f32[4,384,384,4]{2,1,3,0:T(8,128)} %fusion.86, f32[4,384,384,4]{2,1,3,0:T(8,128)} %get-tuple-element.16, f32[4,4,384]{2,1,0:T(4,128)S(1)} %get-tuple-element.15, pred[384,384]{0,1:T(8,128)(4,1)S(1)} %iota_compare_fusion), kind=kOutput, calls=%fused_computation.16 | convolution fusion | flops 327948672 | bytes 20815872 | tf_op jit(solution)/shard_map/kgtu,ukd->tkgd/dot_general | solution.py:57
  182.5 1.5 bitcast_multiply_fusion.8
  184.0 0.1 slice_negate_fusion
  184.2 0.1 pad_maximum_fusion
  184.3 1.2 copy-done.3
  185.4 1.2 fusion.34
  186.6 6.0 %fusion.60 = bf16[4,64,384]{2,1,0:T(8,128)(2,1)S(1)} fusion(bf16[384,4,4,64]{0,3,2,1:T(8,128)(2,1)S(1)} %bitcast.179, f32[4,384,384,4]{2,1,3,0:T(8,128)} %get-tuple-element.16, f32[4,4,384]{2,1,0:T(4,128)S(1)} %get-tuple-element.15, pred[384,384]{0,1:T(8,128)(4,1)S(1)} %iota_compare_fusion), kind=kOutput, calls=%fused_computation.66 | convolution fusion | flops 311525376 | bytes 10592256 | tf_op jit(solution)/shard_map/kgtu,tkgd->ukd/dot_general | solution.py:57
  192.6 0.0 reduce-scatter.6.cloned.1.call-done
  192.7 0.0 reduce-scatter.8.cloned.1.call-update
  192.7 14.2 %broadcast_multiply_fusion = (f32[384,4,64]{0,2,1:T(8,128)S(1)}, f32[384,4,64]{0,2,1:T(8,128)S(1)}) fusion(f32[384,64]{0,1:T(8,128)S(1)} %get-tuple-element.12, bf16[384,4,4,64]{0,3,2,1:T(8,128)(2,1)S(1)} %copy-done.6, f32[4,384,384,4]{2,1,3,0:T(8,128)} %fusion.86, f32[4,4,384]{2,1,0:T(4,128)S(1)} %get-tuple-element.15, ...), kind=kOutput, calls=%fused_computation.83 | convolution fusion | flops 328046976 | bytes 20717568 | tf_op jit(solution)/shard_map/kgtu,tkgd->ukd/dot_general | solution.py:57
  207.0 0.1 fusion.68
  207.1 6.3 %fusion.23 = (f32[384]{0:T(512)S(1)}, f32[384,2048]{1,0:T(8,128)S(1)}) fusion(bf16[1,2,384,2048]{3,2,1,0:T(8,128)(2,1)} %param.9, s32[]{:T(128)S(6)} %select_n.17, f32[2048]{0:T(1024)S(1)} %bitcast.190, bf16[2048,1536]{1,0:T(8,128)(2,1)} %bitcast.6, bf16[384,256]{0,1:T(8,128)(2,1)S(1)} %bitcast.191, bf16[384,256]{0,1:T(8,128)(2,1)S(1)} %bitcast.187, ...), kind=kOutput, calls=%fused_computation.32 | convolution fusion | flops 2422603264 | bytes 12199428 | tf_op jit(solution)/shard_map/dot_general | solution.py:148
  213.4 0.8 fusion.22
  214.2 1.0 collective-permute-start
  215.2 43.0 %collective-permute-done = bf16[384,2048]{1,0:T(8,128)(2,1)} collective-permute-done((bf16[384,2048]{1,0:T(8,128)(2,1)S(1)}, bf16[384,2048]{1,0:T(8,128)(2,1)}, u32[]{:S(2)}, u32[]{:S(2)}) %collective-permute-start) | collective-permute-done | bytes 1572896 | tf_op jit(solution)/shard_map/ppermute | solution.py:17
  258.3 2.0 bitcast_convert_fusion
  260.2 50.2 %reduce-scatter.8.cloned.1.call-done = bf16[1,64,2048]{2,1,0:T(8,128)(2,1)} async-done(((bf16[8,64,2048]{2,1,0:T(8,128)(2,1)}), bf16[1,64,2048]{2,1,0:T(8,128)(2,1)}) %reduce-scatter.8.cloned.1.call-update) | async-done | bytes 262160 | tf_op jit(solution)/shard_map/reduce_scatter | solution.py:31
  310.4 1.8 convert_element_type.82
  312.2 2.7 copy.44
  (30 shorter events, 0.3 us)
Async XLA Ops:
  8.0 22.5 %copy-start = (bf16[1,2,384,1536]{3,2,1,0:T(8,128)(2,1)S(1)}, bf16[1,2,384,1536]{3,2,1,0:T(8,128)(2,1)}, u32[]{:S(2)}) copy-start(bf16[1,2,384,1536]{3,2,1,0:T(8,128)(2,1)} %param.12) | copy-start | bytes 7077892
  8.0 148.3 %all-gather.3.cloned.1.call-start = ((), (), s32[]{:S(2)}) async-start(), calls=%async_computation.7 | async-start | bytes 4456448 | tf_op jit(solution)/shard_map/all_gather | solution.py:143
  8.7 183.9 %reduce-scatter.6.cloned.1.call-start = ((), (), s32[]{:S(2)}) async-start(), calls=%async_computation.5 | async-start | bytes 6291456 | tf_op jit(solution)/shard_map/reduce_scatter | solution.py:30
  15.8 1.0 copy-start.8
  20.0 10.5 %copy-start.9 = (f32[1,2048]{1,0:T(1,128)S(1)}, f32[1,2048]{1,0:T(1,128)}, u32[]{:S(2)}) copy-start(f32[1,2048]{1,0:T(1,128)} %param.15) | copy-start | bytes 24580
  20.0 120.2 %all-to-all-start = ((bf16[16,128,1536]{2,1,0:T(8,128)(2,1)}), bf16[16,128,1536]{2,1,0:T(8,128)(2,1)}, u32[]{:S(2)}, u32[]{:S(2)}) async-start(bf16[16,128,1536]{2,1,0:T(8,128)(2,1)} %stack.3), calls=%async_computation | async-start | bytes 12582912 | tf_op jit(solution)/shard_map/all_to_all | solution.py:139
  28.6 229.7 %reduce-scatter.4.cloned.1.call-start = ((), (), s32[]{:S(2)}) async-start(), calls=%async_computation.4 | async-start | bytes 6684672 | tf_op jit(solution)/shard_map/reduce_scatter | solution.py:159
  38.2 272.3 %reduce-scatter.8.cloned.1.call-start = ((), (), s32[]{:S(2)}) async-start(), calls=%async_computation.6 | async-start | bytes 2359296 | tf_op jit(solution)/shard_map/reduce_scatter | solution.py:31
  149.7 0.9 copy-start.5
  184.0 1.4 copy-start.3
  186.6 6.1 %copy-start.6 = (bf16[384,4,4,64]{0,3,2,1:T(8,128)(2,1)S(1)}, bf16[384,4,4,64]{0,3,2,1:T(8,128)(2,1)}, u32[]{:S(2)}) copy-start(bf16[384,4,4,64]{0,3,2,1:T(8,128)(2,1)} %copy-done.5) | copy-start | bytes 2359300
  192.7 14.4 %copy-start.7 = (bf16[384,1024]{0,1:T(8,128)(2,1)S(1)}, bf16[384,1024]{0,1:T(8,128)(2,1)}, u32[]{:S(2)}) copy-start(bf16[384,1024]{0,1:T(8,128)(2,1)} %fusion.34) | copy-start | bytes 2359300
  207.1 6.3 %copy-start.2 = (bf16[1,2,384,2048]{3,2,1,0:T(8,128)(2,1)S(1)}, bf16[1,2,384,2048]{3,2,1,0:T(8,128)(2,1)}, u32[]{:S(2)}) copy-start(bf16[1,2,384,2048]{3,2,1,0:T(8,128)(2,1)} %param.9) | copy-start | bytes 9437188
  207.1 6.3 %copy-start.4 = (bf16[1,2,384,2048]{3,2,1,0:T(8,128)(2,1)S(1)}, bf16[1,2,384,2048]{3,2,1,0:T(8,128)(2,1)}, u32[]{:S(2)}) copy-start(bf16[1,2,384,2048]{3,2,1,0:T(8,128)(2,1)} %param.10) | copy-start | bytes 9437188
  213.4 101.5 %copy-start.1 = (bf16[1,2,384,1536]{3,2,1,0:T(8,128)(2,1)S(1)}, bf16[1,2,384,1536]{3,2,1,0:T(8,128)(2,1)}, u32[]{:S(2)}) copy-start(bf16[1,2,384,1536]{3,2,1,0:T(8,128)(2,1)} %param.12) | copy-start | bytes 7077892
  214.2 44.0 %collective-permute-start = (bf16[384,2048]{1,0:T(8,128)(2,1)S(1)}, bf16[384,2048]{1,0:T(8,128)(2,1)}, u32[]{:S(2)}, u32[]{:S(2)}) collective-permute-start(bf16[384,2048]{1,0:T(8,128)(2,1)S(1)} %fusion.22), channel_id=1, source_target_pairs={{0,240},{16,0},{32,16},{48,32},{64,48},{80,64},{96,80},{112,96},{1... | collective-permute-start | bytes 4718600 | tf_op jit(solution)/shard_map/ppermute | solution.py:17
Sparse Core Ops, SparseCore 0:
  11.6 141.8 all-gather.2
Sparse Core Ops, SparseCore 1:
  15.9 21.8 reduce-scatter.5
  42.1 129.5 reduce-scatter.3
  192.8 117.6 reduce-scatter.7
